TPU v7x, 128 devices: a whole 4x4x4 slice. The times are simulated.
128 devices in a mesh: fsdp: 32 (over x_hi, z, y), tensor: 4 (over x_lo, core).
Axes of the slice: x: 4 (x_hi: 2, x_lo: 2; x = x_hi * 2 + x_lo), y: 4, z: 4, core: 2. Of those that a mesh axis runs over, the one named last changes fastest.
Arguments:
- activations: bfloat16 [32768, 5120], P('fsdp', 'tensor'), may hold values from -6 to 6
- cotangent: bfloat16 [32768, 5120], P('fsdp', 'tensor'), may hold values from -0.032958984 to 0.032958984
- weights: float32 [5120, 5120], P(None, ('tensor', 'fsdp')), may hold values from -0.025 to 0.025
- first_moment: float32 [5120, 5120], P(None, ('tensor', 'fsdp')), may hold values from -3 to 3
- second_moment: float32 [5120, 5120], P(None, ('tensor', 'fsdp')), may hold values from 0.01 to 1
Outputs:
- weights_new: float32 [5120, 5120], P('fsdp', 'tensor')
- first_new: float32 [5120, 5120], P('fsdp', 'tensor')
- second_new: float32 [5120, 5120], P('fsdp', 'tensor')
- weights_bf16: bfloat16 [5120, 5120], P(None, 'tensor')
All inputs are finite; a program needn't handle non-finite values.
Results may differ from a plain program's by a relative error of at most 0.014.
Values may be sent and summed in bfloat16 or wider, within the bound.
A program may use at most 128 MiB of HBM per device.

v0:
```python
import jax
import jax.numpy as jnp
from jax import lax
from jax.sharding import PartitionSpec as P

STEP = 20


beta_one = 0.9
beta_two = 0.95
adam_eps = 1e-08
learn_rate = 0.0003
decay_rate = 0.1


def split_up(value, dim, count):
    before, after = (value.shape[:dim], value.shape[dim + 1 :])
    return jnp.moveaxis(value.reshape(*before, count, -1, *after), dim, 0)


def sent_and_summed(value, axis, dim):
    count = lax.axis_size(axis)
    parts = lax.all_to_all(split_up(value, dim, count), axis, 0, 0, tiled=True)
    return jnp.sum(parts.astype(jnp.float32), axis=0)


def adam_update(weights, first_moment, second_moment, gradient):
    first_new = beta_one * first_moment + (1.0 - beta_one) * gradient
    second_new = beta_two * second_moment + (1.0 - beta_two) * gradient * gradient
    corrected = first_new / (1.0 - beta_one**STEP)
    scaled = jnp.sqrt(second_new / (1.0 - beta_two**STEP)) + adam_eps
    weights_new = weights - learn_rate * (corrected / scaled + decay_rate * weights)
    return (weights_new, first_new, second_new)


def body(activations, cotangent, weights, first_moment, second_moment):
    gathered = lax.all_gather(activations, "tensor", axis=1, tiled=True)
    transposed = sent_and_summed(
        lax.dot_general(
            cotangent, gathered, (((0,), (0,)), ((), ())), preferred_element_type=jnp.float32
        ).astype(jnp.bfloat16),
        "fsdp",
        0,
    )
    gradient = transposed.T
    weights_old, first_old, second_old = adam_update(weights, first_moment, second_moment, gradient)
    weights_bf16 = lax.all_gather(weights_old.astype(jnp.bfloat16), "fsdp", axis=1, tiled=True)
    weights_new, first_new, second_new = (
        lax.all_to_all(
            weights_old.astype(jnp.bfloat16), "fsdp", split_axis=0, concat_axis=1, tiled=True
        ).astype(weights_old.dtype),
        lax.all_to_all(
            first_old.astype(jnp.bfloat16), "fsdp", split_axis=0, concat_axis=1, tiled=True
        ).astype(first_old.dtype),
        lax.all_to_all(
            second_old.astype(jnp.bfloat16), "fsdp", split_axis=0, concat_axis=1, tiled=True
        ).astype(second_old.dtype),
    )
    return (weights_new, first_new, second_new, weights_bf16)


def solution(mesh):
    return jax.shard_map(
        body,
        mesh=mesh,
        in_specs=(
            P("fsdp", "tensor"),
            P("fsdp", "tensor"),
            P(None, ("tensor", "fsdp")),
            P(None, ("tensor", "fsdp")),
            P(None, ("tensor", "fsdp")),
        ),
        out_specs=(
            P("fsdp", "tensor"),
            P("fsdp", "tensor"),
            P("fsdp", "tensor"),
            P(None, "tensor"),
        ),
        check_vma=False,
    )
```

profile of v0, /device:TPU:2, one launch (start us, length us, event | category | flops | bytes accessed | tf_op | source)
XLA Modules:
  0.0 468.7 jit_solution(9544911949169199346)
XLA Ops:
  7.2 0.7 all-gather.3.cloned.1.call-update
  8.0 101.2 %all-gather.3.cloned.1.call-done = bf16[1024,5120]{1,0:T(8,128)(2,1)} async-done(((bf16[1024,1280]{1,0:T(8,128)(2,1)}), bf16[1024,5120]{1,0:T(8,128)(2,1)}) %all-gather.3.cloned.1.call-update) | async-done | bytes 10485776 | tf_op jit(solution)/shard_map/all_gather | solution.py:37
  109.1 20.2 %convolution_convert_fusion = bf16[1280,5120]{1,0:T(8,128)(2,1)} fusion(bf16[1024,1280]{1,0:T(8,128)(2,1)S(1)} %copy-done, bf16[1024,5120]{1,0:T(8,128)(2,1)} %all-gather.3.cloned.1.call-done), kind=kOutput, calls=%fused_computation.1 | convolution fusion | flops 13428326400 | bytes 26214400 | tf_op jit(solution)/shard_map/dot_general | solution.py:39
  129.3 159.9 %all_to_all.44 = bf16[32,40,5120]{2,1,0:T(8,128)(2,1)} all-to-all(bf16[32,40,5120]{2,1,0:T(8,128)(2,1)} %bitcast.31), channel_id=1, replica_groups=mesh['fsdp'=32,'tensor'=4] {'fsdp'}, dimensions={0} | all-to-all | bytes 26214400 | tf_op jit(solution)/shard_map/all_to_all | solution.py:23
  289.2 7.7 %convert_reduce_fusion = f32[40,5120]{1,0:T(8,128)S(1)} fusion(bf16[32,40,5120]{2,1,0:T(8,128)(2,1)} %all_to_all.44), kind=kLoop, calls=%fused_computation | loop fusion | flops 12902400 | bytes 13926400 | tf_op jit(solution)/shard_map/reduce_sum | solution.py:24
  296.9 2.6 fusion.3
  299.5 0.8 all_to_all.38
  300.3 1.2 copy.28
  301.5 9.5 %all-to-all-start.3 = ((bf16[32,160,40]{1,2,0:T(8,128)(2,1)}), bf16[32,160,40]{1,2,0:T(8,128)(2,1)S(1)}, u32[]{:S(2)}, u32[]{:S(2)}) async-start(bf16[32,160,40]{1,2,0:T(8,128)(2,1)} %copy.28), calls=%async_computation.3 | async-start | bytes 1310720 | tf_op jit(solution)/shard_map/all_to_all | solution.py:55
  311.0 0.8 all_to_all.36
  311.9 1.2 copy.27
  313.1 15.4 %all-to-all-done.3 = bf16[32,160,40]{1,2,0:T(8,128)(2,1)S(1)} async-done(((bf16[32,160,40]{1,2,0:T(8,128)(2,1)}), bf16[32,160,40]{1,2,0:T(8,128)(2,1)S(1)}, u32[]{:S(2)}, u32[]{:S(2)}) %all-to-all-start.3) | async-done | bytes 409632 | tf_op jit(solution)/shard_map/all_to_all | solution.py:55
  328.4 4.3 all-to-all-start.2
  332.7 1.8 all_to_all.34
  334.5 1.2 copy.26
  335.7 14.1 %all-to-all-done.2 = bf16[32,160,40]{1,2,0:T(8,128)(2,1)S(1)} async-done(((bf16[32,160,40]{1,2,0:T(8,128)(2,1)}), bf16[32,160,40]{1,2,0:T(8,128)(2,1)S(1)}, u32[]{:S(2)}, u32[]{:S(2)}) %all-to-all-start.2) | async-done | bytes 409632 | tf_op jit(solution)/shard_map/all_to_all | solution.py:52
  349.8 4.7 all-to-all-start.1
  354.6 1.3 copy.31
  356.0 1.3 copy.30
  357.2 10.4 %all-to-all-done.1 = bf16[32,160,40]{1,2,0:T(8,128)(2,1)S(1)} async-done(((bf16[32,160,40]{1,2,0:T(8,128)(2,1)}), bf16[32,160,40]{1,2,0:T(8,128)(2,1)S(1)}, u32[]{:S(2)}, u32[]{:S(2)}) %all-to-all-start.1) | async-done | bytes 409632 | tf_op jit(solution)/shard_map/all_to_all | solution.py:49
  367.7 1.2 convert_element_type.60
  368.8 2.7 copy.29
  371.6 72.7 %all-gather.5.cloned.1.call-done = bf16[5120,1280]{0,1:T(8,128)(2,1)} async-done(((bf16[5120,40]{0,1:T(8,128)(2,1)}), bf16[5120,1280]{0,1:T(8,128)(2,1)}) %all-gather.5.cloned.1.call-update) | async-done | bytes 13107216 | tf_op jit(solution)/shard_map/all_gather | solution.py:47
  444.2 17.6 %copy.32 = bf16[5120,1280]{1,0:T(8,128)(2,1)} copy(bf16[5120,1280]{0,1:T(8,128)(2,1)} %all-gather.5.cloned.1.call-done) | data formatting | bytes 26214400
  (13 shorter events, 0.3 us)
Async XLA Ops:
  7.2 102.0 %copy-start = (bf16[1024,1280]{1,0:T(8,128)(2,1)S(1)}, bf16[1024,1280]{1,0:T(8,128)(2,1)}, u32[]{:S(2)}) copy-start(bf16[1024,1280]{1,0:T(8,128)(2,1)} %param.6) | copy-start | bytes 7864324
  7.2 102.0 %all-gather.3.cloned.1.call-start = ((), (), s32[]{:S(2)}) async-start(), calls=%async_computation.4 | async-start | bytes 13107200 | tf_op jit(solution)/shard_map/all_gather | solution.py:37
  7.9 436.3 %all-gather.5.cloned.1.call-start = ((), (), s32[]{:S(2)}) async-start(), calls=%async_computation.5 | async-start | bytes 13516800 | tf_op jit(solution)/shard_map/all_gather | solution.py:47
  289.2 7.7 %copy-start.2 = (f32[5120,40]{0,1:T(8,128)S(1)}, f32[5120,40]{0,1:T(8,128)}, u32[]{:S(2)}) copy-start(f32[5120,40]{0,1:T(8,128)} %param.9) | copy-start | bytes 2457604
  289.2 7.7 %copy-start.3 = (f32[5120,40]{0,1:T(8,128)S(1)}, f32[5120,40]{0,1:T(8,128)}, u32[]{:S(2)}) copy-start(f32[5120,40]{0,1:T(8,128)} %param.7) | copy-start | bytes 2457604
  301.5 26.9 %all-to-all-start.3 = ((bf16[32,160,40]{1,2,0:T(8,128)(2,1)}), bf16[32,160,40]{1,2,0:T(8,128)(2,1)S(1)}, u32[]{:S(2)}, u32[]{:S(2)}) async-start(bf16[32,160,40]{1,2,0:T(8,128)(2,1)} %copy.28), calls=%async_computation.3 | async-start | bytes 1310720 | tf_op jit(solution)/shard_map/all_to_all | solution.py:55
  328.4 21.4 %all-to-all-start.2 = ((bf16[32,160,40]{1,2,0:T(8,128)(2,1)}), bf16[32,160,40]{1,2,0:T(8,128)(2,1)S(1)}, u32[]{:S(2)}, u32[]{:S(2)}) async-start(bf16[32,160,40]{1,2,0:T(8,128)(2,1)} %copy.27), calls=%async_computation.2 | async-start | bytes 1310720 | tf_op jit(solution)/shard_map/all_to_all | solution.py:52
  349.8 17.9 %all-to-all-start.1 = ((bf16[32,160,40]{1,2,0:T(8,128)(2,1)}), bf16[32,160,40]{1,2,0:T(8,128)(2,1)S(1)}, u32[]{:S(2)}, u32[]{:S(2)}) async-start(bf16[32,160,40]{1,2,0:T(8,128)(2,1)} %copy.26), calls=%async_computation.1 | async-start | bytes 1310720 | tf_op jit(solution)/shard_map/all_to_all | solution.py:49
  368.8 93.0 %copy-start.1 = (bf16[1024,1280]{1,0:T(8,128)(2,1)S(1)}, bf16[1024,1280]{1,0:T(8,128)(2,1)}, u32[]{:S(2)}) copy-start(bf16[1024,1280]{1,0:T(8,128)(2,1)} %param.6) | copy-start | bytes 7864324
Sparse Core Ops, SparseCore 0:
  9.6 99.4 all-gather.2
  299.6 144.5 all-gather.4
where the time goes:
time: 471 us; the launch traced here: 469 us
  waiting for transfers between devices  214 us (45%)
  blocking collectives  160 us (34%)
  local copies, waits for them, and re-layouts  29.9 us (6%)
  matrix products  20.2 us (4%)
  starting transfers between devices  18.6 us (4%)
  between operations  14.1 us (3%)
  other arithmetic  11.6 us (2%)
    all_to_all x1, blocking collectives, sent_and_summed(): parts = lax.all_to_all(split_up(value, dim, count), axis, 0, 0, tiled=True)  160 us
    all_gather x1, waiting for transfers between devices, body(): gathered = lax.all_gather(activations, 'tensor', axis=1, tiled=True)  101 us
    all_gather x1, waiting for transfers between devices, body(): lax.all_gather(weights_old.astype(jnp.bfloat16), 'fsdp', axis=1, tiled=True)  72.7 us
    unnamed x12, local copies, waits for them, and re-layouts  22.9 us
    dot_general x1, matrix products, body(): lax.dot_general(cotangent, gathered, (((0,), (0,)), ((), ())), preferred_...  20.2 us
    all_to_all x1, waiting for transfers between devices, body(): lax.all_to_all(second_old.astype(jnp.bfloat16), 'fsdp', split_axis=0, con...  15.4 us
    all_to_all x1, waiting for transfers between devices, body(): lax.all_to_all(first_old.astype(jnp.bfloat16), 'fsdp', split_axis=0, conc...  14.1 us
    all_to_all x1, waiting for transfers between devices, body(): lax.all_to_all(weights_old.astype(jnp.bfloat16), 'fsdp', split_axis=0, co...  10.4 us
  transfers between devices with their start and end apart: 5, of which 5 were waited for; matrix products, arithmetic and copies ran while one was open for 2% of the time, Pallas kernels for 0%

commit v1 on v0

v1 whole, which is shorter than its diff:
```python
import jax
import jax.numpy as jnp
from jax import lax
from jax.experimental import pallas as pl
from jax.experimental.pallas import tpu as pltpu
from jax.sharding import PartitionSpec as P

STEP = 20
D = 5120
BLOCK = 160
WAVES = 10
WIDE = 256
MESH = pl.DeviceIdType.MESH
BF = jnp.bfloat16

beta_one = 0.9
beta_two = 0.95
adam_eps = 1e-08
learn_rate = 0.0003
decay_rate = 0.1

ORDER = ((0, 2, 1, 3), (1, 3, 0, 2), (2, 1, 3, 0), (3, 0, 2, 1))
SLOT = (0, 8, 12, 14)


def adam_update(weights, first_moment, second_moment, gradient):
    first_new = beta_one * first_moment + (1.0 - beta_one) * gradient
    second_new = beta_two * second_moment + (1.0 - beta_two) * gradient * gradient
    corrected = first_new / (1.0 - beta_one**STEP)
    scaled = jnp.sqrt(second_new / (1.0 - beta_two**STEP)) + adam_eps
    weights_new = weights - learn_rate * (corrected / scaled + decay_rate * weights)
    return (weights_new, first_new, second_new)


def flip(value, dim):
    return value + 1 - 2 * (value % 2) if dim % 2 == 0 else 3 - value


def cube_bits(z, y):
    return ((y + y // 2) % 2, y // 2, (z + z // 2) % 2, z // 2)


def place(color, z, y):
    bits = cube_bits(z, y)
    order = ORDER[color]
    return bits[order[0]] * 8 + bits[order[1]] * 4 + bits[order[2]] * 2 + bits[order[3]]


def kernel(
    at_ref, c_ref, state_ref, wn_out, mn_out, vn_out, full_out,
    at, cot, part, recv, summed, final, full, state, fresh,
    load_sem, a_send, a_recv, c_send, c_recv, rs_send, rs_recv, x_send, x_recv, ag_send, ag_recv,
    gx_send, gx_recv, out_sem,
):
    f, t = lax.axis_index("fsdp"), lax.axis_index("tensor")
    hi, z, y = f // 16, (f // 4) % 4, f % 4
    lo, core = t // 2, t % 2

    def at_device(hi_, z_, y_, lo_, core_):
        return ((hi_ * 4 + z_) * 4 + y_, lo_ * 2 + core_)

    def cube_peer(dim):
        if dim < 2:
            return at_device(hi, z, flip(y, dim), lo, core)
        return at_device(hi, flip(z, dim), y, lo, core)

    def remote(src, dst, send, receive, device):
        return pltpu.make_async_remote_copy(
            src_ref=src, dst_ref=dst, send_sem=send, recv_sem=receive, device_id=device, device_id_type=MESH
        )

    bits = cube_bits(z, y)
    core_peer = at_device(hi, z, y, lo, 1 - core)
    lo_peer = at_device(hi, z, y, 1 - lo, core)
    hi_peer = at_device(1 - hi, z, y, lo, core)
    across = at_device(1 - hi, z, y, 1 - lo, core)

    barrier = pltpu.get_barrier_semaphore()
    greeted = [cube_peer(dim) for dim in range(4)] + [core_peer, lo_peer, hi_peer, across]
    for device in greeted:
        pl.semaphore_signal(barrier, inc=1, device_id=device, device_id_type=MESH)
    pl.semaphore_wait(barrier, len(greeted))

    mine = pl.ds(pl.multiple_of(core * 1280, 128), 1280)
    send_a = remote(at_ref, at.at[mine], a_send, a_recv, core_peer)
    send_a.start()
    load_a = pltpu.make_async_copy(at_ref, at.at[mine], load_sem.at[0])
    load_a.start()
    load_c = [
        pltpu.make_async_copy(c_ref.at[:, pl.ds(WIDE * k, WIDE)], cot.at[k], load_sem.at[1 + k]) for k in range(5)
    ]
    for k in range(5):
        load_c[k].start()
    send_c = [
        remote(c_ref.at[:, pl.ds(WIDE * k, WIDE)], cot.at[5 + k], c_send.at[k], c_recv.at[k], lo_peer)
        for k in range(5)
    ]
    for k in range(5):
        send_c[k].start()
    load_s = pltpu.make_async_copy(state_ref, state, load_sem.at[6])
    load_s.start()
    load_a.wait()
    for k in range(5):
        load_c[k].wait()
    load_s.wait()
    send_a.wait_recv()

    def base(color, stage):
        total = 0
        for s in range(stage):
            total = total + bits[ORDER[color][s]] * (8 >> s)
        return total

    def halving(wave, color, stage):
        half = 8 >> stage
        dim = ORDER[color][stage]
        return remote(
            part.at[wave, color, pl.ds(base(color, stage) + (1 - bits[dim]) * half, half)],
            recv.at[wave, color, pl.ds(SLOT[stage], half)],
            rs_send,
            rs_recv.at[wave, stage, color],
            cube_peer(dim),
        )

    def add(wave, color, stage, which):
        half = 8 >> stage
        bit = bits[ORDER[color][stage]]
        shift = (1 - bit if which else bit) * half
        own = pl.ds(base(color, stage) + shift, half)
        came = pl.ds(SLOT[stage - 1] + shift, half)
        part[wave, color, own] = (
            part[wave, color, own].astype(jnp.float32) + recv[wave, color, came].astype(jnp.float32)
        ).astype(BF)

    def x_target(wave):
        column = jnp.where(wave < 5, lo, 1 - lo)
        return at_device(lo, z, y, column, core)

    def x_copy(wave):
        k = wave % 5
        return remote(summed.at[wave], final.at[hi, k], x_send.at[wave], x_recv.at[hi, k], x_target(wave))

    stays = hi == lo

    def tick(now, carry):
        wave_4 = now - 5

        @pl.when((wave_4 >= 0) & (wave_4 < WAVES))
        def _():
            for color in range(4):
                halving(wave_4, color, 3).wait_recv()
                summed[wave_4, color] = (
                    part[wave_4, color, base(color, 4)].astype(jnp.float32)
                    + recv[wave_4, color, SLOT[3]].astype(jnp.float32)
                ).astype(BF)

            @pl.when(stays & (wave_4 < 5))
            def _():
                final[hi, wave_4 % 5] = summed[wave_4]

            @pl.when(jnp.logical_not(stays & (wave_4 < 5)))
            def _():
                x_copy(wave_4).start()

        for stage in (3, 2, 1):
            wave = now - 1 - stage

            @pl.when((wave >= 0) & (wave < WAVES))
            def _(wave=wave, stage=stage):
                for color in range(4):
                    halving(wave, color, stage - 1).wait_recv()
                    add(wave, color, stage, 1)
                    halving(wave, color, stage).start()
                    add(wave, color, stage, 0)

        @pl.when(now < WAVES)
        def _():
            for k in range(5):
                @pl.when(now == 5 + k)
                def _(k=k):
                    send_c[k].wait_recv()

            def rows(quarter, carry):
                left = at[pl.ds(pl.multiple_of(quarter * 640, 128), 640), :]
                product = jnp.dot(left, cot[now], preferred_element_type=jnp.float32).astype(BF)
                for i in range(4):
                    for color in range(4):
                        top, side = i * BLOCK + (color // 2) * 80, (color % 2) * 128
                        part[now, color, place(color, quarter, i)] = product[top : top + 80, side : side + 128]
                return carry

            lax.fori_loop(0, 4, rows, 0)
            for color in range(4):
                halving(now, color, 0).start()

        return carry

    lax.fori_loop(0, WAVES + 5, tick, 0)

    my_rows = pl.multiple_of(f * BLOCK, BLOCK)

    def update(k, carry):
        for source in range(2):
            @pl.when(jnp.logical_not(stays & (hi == source)))
            def _(source=source):
                pltpu.make_async_copy(final.at[source, k], final.at[source, k], x_recv.at[source, k]).wait()

        for color in range(4):
            rows = pl.ds((color // 2) * 80, 80)
            columns = pl.ds(pl.multiple_of(k * WIDE + (color % 2) * 128, 128), 128)
            gradient = final[0, k, color].astype(jnp.float32) + final[1, k, color].astype(jnp.float32)
            new = adam_update(*(state[i, rows, columns].astype(jnp.float32) for i in range(3)), gradient)
            for i in range(3):
                fresh[i, rows, columns] = new[i]
            full[pl.ds(my_rows + (color // 2) * 80, 80), columns] = new[0].astype(BF)
        return carry

    lax.fori_loop(0, 5, update, 0)

    def block(x, color, number):
        z_, y_ = z, y
        order = ORDER[color][::-1]
        for i in range(4):
            if number >> i & 1:
                dim = order[i]
                if dim < 2:
                    y_ = flip(y_, dim)
                else:
                    z_ = flip(z_, dim)
        owner = ((1 - hi if x else hi) * 4 + z_) * 4 + y_
        rows = pl.ds(pl.multiple_of(owner * BLOCK + (color // 2) * 80, 16), 80)
        return full.at[rows, pl.ds((color % 2) * 640, 640)]

    def forward(x, color, number, i):
        here = block(x, color, number)
        return remote(
            here, here, ag_send, ag_recv.at[x, color, number + (1 << i)], cube_peer(ORDER[color][::-1][i])
        )

    def arrived(x, color, number):
        here = block(x, color, number)
        pltpu.make_async_copy(here, here, ag_recv.at[x, color, number]).wait()

    own_rows = full.at[pl.ds(my_rows, BLOCK)]
    to_hi = remote(own_rows, own_rows, gx_send, gx_recv, hi_peer)
    to_hi.start()
    for color in range(4):
        for i in (3, 2, 1, 0):
            forward(0, color, 0, i).start()
    stores = [
        pltpu.make_async_copy(fresh.at[i], out, out_sem.at[i]) for i, out in enumerate((wn_out, mn_out, vn_out))
    ]
    for store in stores:
        store.start()
    for number in range(1, 8):
        for color in range(4):
            arrived(0, color, number)
            for i in (3, 2, 1):
                if number < 1 << i:
                    forward(0, color, number, i).start()
    to_hi.wait_recv()
    for color in range(4):
        for i in (3, 2, 1, 0):
            forward(1, color, 0, i).start()
    for number in range(8, 16):
        for color in range(4):
            arrived(0, color, number)
    near = pl.ds(pl.multiple_of(hi * 2560, 128), 2560)
    far = pl.ds(pl.multiple_of((1 - hi) * 2560, 128), 2560)
    store_near = pltpu.make_async_copy(full.at[near], full_out.at[near], out_sem.at[3])
    store_near.start()
    for number in range(1, 8):
        for color in range(4):
            arrived(1, color, number)
            for i in (3, 2, 1):
                if number < 1 << i:
                    forward(1, color, number, i).start()
    for number in range(8, 16):
        for color in range(4):
            arrived(1, color, number)
    store_far = pltpu.make_async_copy(full.at[far], full_out.at[far], out_sem.at[4])
    store_far.start()

    send_a.wait_send()
    for k in range(5):
        send_c[k].wait_send()
    pltpu.make_async_copy(recv, recv, rs_send).wait()
    for wave in range(WAVES):
        if wave < 5:
            @pl.when(jnp.logical_not(stays))
            def _(wave=wave):
                x_copy(wave).wait_send()
        else:
            x_copy(wave).wait_send()
    to_hi.wait_send()
    pltpu.make_async_copy(full.at[pl.ds(0, 4800)], full.at[pl.ds(0, 4800)], ag_send).wait()
    for store in stores:
        store.wait()
    store_near.wait()
    store_far.wait()


def body(activations, cotangent, weights, first_moment, second_moment):
    packed = jnp.concatenate([weights, first_moment, second_moment], axis=1).astype(BF)
    moved = lax.all_to_all(packed.reshape(32, BLOCK, 120), "fsdp", 0, 0, tiled=True)
    state = moved.reshape(32, BLOCK, 3, 40).transpose(2, 1, 0, 3).reshape(3, BLOCK, 1280)
    any_space = pl.BlockSpec(memory_space=pl.ANY)
    shard = jax.ShapeDtypeStruct((BLOCK, 1280), jnp.float32)
    dma = pltpu.SemaphoreType.DMA
    return pl.pallas_call(
        kernel,
        name="step",
        out_shape=(shard, shard, shard, jax.ShapeDtypeStruct((D, 1280), BF)),
        in_specs=[any_space] * 3,
        out_specs=(any_space,) * 4,
        scratch_shapes=[
            pltpu.VMEM((2560, 1024), BF),
            pltpu.VMEM((10, 1024, WIDE), BF),
            pltpu.VMEM((WAVES, 4, 16, 80, 128), BF),
            pltpu.VMEM((WAVES, 4, 15, 80, 128), BF),
            pltpu.VMEM((WAVES, 4, 80, 128), BF),
            pltpu.VMEM((2, 5, 4, 80, 128), BF),
            pltpu.VMEM((D, 1280), BF),
            pltpu.VMEM((3, BLOCK, 1280), BF),
            pltpu.VMEM((3, BLOCK, 1280), jnp.float32),
            dma((7,)), dma, dma, dma((5,)), dma((5,)), dma, dma((WAVES, 4, 4)), dma((WAVES,)), dma((2, 5)),
            dma, dma((2, 4, 16)), dma, dma, dma((5,)),
        ],
        compiler_params=pltpu.CompilerParams(
            collective_id=0, has_side_effects=True, vmem_limit_bytes=67043328
        ),
        cost_estimate=pl.CostEstimate(flops=13_421_772_800, bytes_accessed=40_000_000, transcendentals=0),
    )(activations.T, cotangent, state)


def solution(mesh):
    return jax.shard_map(
        body,
        mesh=mesh,
        in_specs=(
            P("fsdp", "tensor"),
            P("fsdp", "tensor"),
            P(None, ("tensor", "fsdp")),
            P(None, ("tensor", "fsdp")),
            P(None, ("tensor", "fsdp")),
        ),
        out_specs=(
            P("fsdp", "tensor"),
            P("fsdp", "tensor"),
            P("fsdp", "tensor"),
            P(None, "tensor"),
        ),
        check_vma=False,
    )
```

time: 471 us -> 231 us (0.49)
  waiting for transfers between devices: 214 us -> 16 us
  Pallas kernels: 0 us -> 167 us
  blocking collectives: 160 us -> 0 us
  matrix products: 20.2 us -> 0 us
  between operations: 14.1 us -> 0.75 us
  other arithmetic: 11.6 us -> 2.8 us
  starting transfers between devices: 18.6 us -> 9.89 us
    all_gather x2 -> x0, waiting for transfers between devices: 174 us -> none  [the longest x1 101 us: body(): gathered = lax.all_gather(activations, 'tensor', axis=1, tiled=True)]
    pallas_call x0 -> x1, Pallas kernels: none -> 167 us  [body(): pl.pallas_call(kernel, name='step', out_shape=(shard, shard, shard, jax.S...]
    all_to_all x1 -> x0, blocking collectives: 160 us -> none  [sent_and_summed(): parts = lax.all_to_all(split_up(value, dim, count), axis, 0, 0, tiled=True)]
    all_to_all x3 -> x1, waiting for transfers between devices: 39.9 us -> 16 us  [body(): lax.all_to_all(packed.reshape(32, BLOCK, 120), 'fsdp', 0, 0, tiled=True)]
    dot_general x1 -> x0, matrix products: 20.2 us -> none  [body(): lax.dot_general(cotangent, gathered, (((0,), (0,)), ((), ())), preferred_...]
    all_to_all x3 -> x1, starting transfers between devices: 18.5 us -> 9.89 us  [body(): lax.all_to_all(packed.reshape(32, BLOCK, 120), 'fsdp', 0, 0, tiled=True)]
    reduce_sum x1 -> x0, other arithmetic: 7.66 us -> none  [sent_and_summed(): return jnp.sum(parts.astype(jnp.float32), axis=0)]
    concatenate x0 -> x4, local copies, waits for them, and re-layouts: none -> 6.08 us  [body(): jnp.concatenate([weights, first_moment, second_moment], axis=1).astype(BF)]
  transfers between devices with their start and end apart: 5 -> 1, of which waited for: 5 -> 1; matrix products, arithmetic and copies ran while one was open for 2% -> 2% of each run, Pallas kernels for 0% -> 0%
where the time goes in v1:
time: 231 us; the launch traced here: 228 us
  Pallas kernels  167 us (72%)
  local copies, waits for them, and re-layouts  32.4 us (14%)
  waiting for transfers between devices  16 us (7%)
  starting transfers between devices  9.89 us (4%)
  other arithmetic  2.8 us (1%)
    pallas_call x1, Pallas kernels, body(): pl.pallas_call(kernel, name='step', out_shape=(shard, shard, shard, jax.S...  167 us
    unnamed x13, local copies, waits for them, and re-layouts  19.1 us
    all_to_all x1, waiting for transfers between devices, body(): lax.all_to_all(packed.reshape(32, BLOCK, 120), 'fsdp', 0, 0, tiled=True)  16 us
    all_to_all x1, starting transfers between devices, body(): lax.all_to_all(packed.reshape(32, BLOCK, 120), 'fsdp', 0, 0, tiled=True)  9.89 us
    concatenate x4, local copies, waits for them, and re-layouts, body(): jnp.concatenate([weights, first_moment, second_moment], axis=1).astype(BF)  6.08 us
  transfers between devices with their start and end apart: 1, of which 1 were waited for; matrix products, arithmetic and copies ran while one was open for 2% of the time, Pallas kernels for 0%

profile of v1, /device:TPU:2, one launch (start us, length us, event | category | flops | bytes accessed | tf_op | source)
XLA Modules:
  0.0 228.4 jit_solution(10516071185166185317)
XLA Ops:
  0.6 0.0 copy-start
  0.6 1.3 convert.12
  1.9 0.0 copy-start.1
  1.9 0.8 concatenate.11
  2.7 0.0 copy-done
  2.8 0.8 concatenate.12
  3.6 0.0 copy-done.1
  3.7 1.7 concatenate.13
  5.3 1.4 pad_maximum_fusion
  6.8 2.8 %copy.18 = bf16[32,160,120]{2,1,0:T(8,128)(2,1)} copy(bf16[32,160,120]{1,0,2:T(8,128)(2,1)S(1)} %pad_maximum_fusion) | data formatting | bytes 2457600 | tf_op jit(solution)/shard_map/concatenate | solution.py:304
  9.6 9.9 %all-to-all-start = ((bf16[32,160,120]{2,1,0:T(8,128)(2,1)}), bf16[32,160,120]{2,1,0:T(8,128)(2,1)S(1)}, u32[]{:S(2)}, u32[]{:S(2)}) async-start(bf16[32,160,120]{2,1,0:T(8,128)(2,1)} %copy.18), calls=%async_computation | async-start | bytes 2621440 | tf_op jit(solution)/shard_map/all_to_all | solution.py:305
  19.5 4.4 %copy.17 = bf16[1024,1280]{0,1:T(8,128)(2,1)} copy(bf16[1024,1280]{1,0:T(8,128)(2,1)} %param.5) | data formatting | bytes 5242880 | tf_op args[0]
  23.9 16.0 %all-to-all-done = bf16[32,160,120]{2,1,0:T(8,128)(2,1)S(1)} async-done(((bf16[32,160,120]{2,1,0:T(8,128)(2,1)}), bf16[32,160,120]{2,1,0:T(8,128)(2,1)S(1)}, u32[]{:S(2)}, u32[]{:S(2)}) %all-to-all-start) | async-done | bytes 1228832 | tf_op jit(solution)/shard_map/all_to_all | solution.py:305
  39.9 2.1 copy.19
  42.0 1.4 copy.20
  43.4 3.7 %copy.21.state_ref = bf16[3,160,1280]{2,1,0:T(8,128)(2,1)} copy(bf16[3,160,1280]{1,2,0:T(8,128)(2,1)} %bitcast.12) | data formatting | bytes 2457600 | tf_op jit(solution)/shard_map/reshape | solution.py:306
  47.1 166.5 %step.1 = (f32[160,1280]{1,0:T(8,128)}, f32[160,1280]{1,0:T(8,128)}, f32[160,1280]{1,0:T(8,128)}, bf16[5120,1280]{1,0:T(8,128)(2,1)}) custom-call(bf16[1280,1024]{1,0:T(8,128)(2,1)} %bitcast.13, bf16[1024,1280]{1,0:T(8,128)(2,1)} %c_ref.1, bf16[3,160,1280]{2,1,0:T(8,128)(2,1)} %copy.21.state_ref), custom_call_target="tpu_custom_call" | custom-call | flops 13421772800 | bytes 40000000 | tf_op jit(solution)/shard_map/step/pallas_call | solution.py:310
  213.6 0.0 copy-start.3
  213.6 0.0 copy-start.2
  213.7 2.2 copy.26
  215.9 0.0 copy-done.3
  215.9 0.9 copy.27
  216.8 0.9 copy.28
  217.6 10.7 %copy.29 = bf16[5120,1280]{1,0:T(8,128)(2,1)} copy(bf16[5120,1280]{1,0:T(8,128)(2,1)} %get-tuple-element.11) | data formatting | bytes 26214400
  (3 shorter events, 0.1 us)
Async XLA Ops:
  0.6 2.1 copy-start
  1.9 1.7 copy-start.1
  9.6 30.3 %all-to-all-start = ((bf16[32,160,120]{2,1,0:T(8,128)(2,1)}), bf16[32,160,120]{2,1,0:T(8,128)(2,1)S(1)}, u32[]{:S(2)}, u32[]{:S(2)}) async-start(bf16[32,160,120]{2,1,0:T(8,128)(2,1)} %copy.18), calls=%async_computation | async-start | bytes 2621440 | tf_op jit(solution)/shard_map/all_to_all | solution.py:305
  213.6 2.2 copy-start.3
  213.6 3.1 %copy-start.2 = (f32[160,1280]{1,0:T(8,128)S(1)}, f32[160,1280]{1,0:T(8,128)}, u32[]{:S(2)}) copy-start(f32[160,1280]{1,0:T(8,128)} %get-tuple-element.10) | copy-start | bytes 2457604

commit v2 on v1

--- a/solution.py
+++ b/solution.py
@@ -47,9 +47,9 @@
 
 
 def kernel(
-    at_ref, c_ref, state_ref, wn_out, mn_out, vn_out, full_out,
-    at, cot, part, recv, summed, final, full, state, fresh,
-    load_sem, a_send, a_recv, c_send, c_recv, rs_send, rs_recv, x_send, x_recv, ag_send, ag_recv,
+    a_ref, c_ref, w_ref, m_ref, v_ref, wn_out, mn_out, vn_out, full_out,
+    at, cot, part, recv, summed, final, full, fresh, tall, packed, moved,
+    load_sem, s_send, s_recv, a_send, a_recv, c_send, c_recv, rs_send, rs_recv, x_send, x_recv, ag_send, ag_recv,
     gx_send, gx_recv, out_sem,
 ):
     f, t = lax.axis_index("fsdp"), lax.axis_index("tensor")
@@ -76,16 +76,28 @@
     across = at_device(1 - hi, z, y, 1 - lo, core)
 
     barrier = pltpu.get_barrier_semaphore()
-    greeted = [cube_peer(dim) for dim in range(4)] + [core_peer, lo_peer, hi_peer, across]
-    for device in greeted:
+    for device in (core_peer, lo_peer, across):
         pl.semaphore_signal(barrier, inc=1, device_id=device, device_id_type=MESH)
-    pl.semaphore_wait(barrier, len(greeted))
-
-    mine = pl.ds(pl.multiple_of(core * 1280, 128), 1280)
-    send_a = remote(at_ref, at.at[mine], a_send, a_recv, core_peer)
+
+    def greet(step, carry):
+        pl.semaphore_signal(barrier, inc=1, device_id=((f + step) % 32, t), device_id_type=MESH)
+        return carry
+
+    lax.fori_loop(1, 32, greet, 0)
+    pl.semaphore_wait(barrier, 34)
+
+    near_row = pl.multiple_of(hi * 2560, 128)
+    raw = [full.at[pl.ds(near_row, 1024)], full.at[pl.ds(near_row + 1024, 1024)]]
+    send_a = remote(a_ref, raw[1], a_send, a_recv, core_peer)
+    load_a = pltpu.make_async_copy(a_ref, raw[0], load_sem.at[0])
+    load_a.start()
     send_a.start()
-    load_a = pltpu.make_async_copy(at_ref, at.at[mine], load_sem.at[0])
-    load_a.start()
+    load_s = [
+        pltpu.make_async_copy(ref, tall.at[pl.ds(40 * i, 40)], load_sem.at[6 + i])
+        for i, ref in enumerate((w_ref, m_ref, v_ref))
+    ]
+    for load in load_s:
+        load.start()
     load_c = [
         pltpu.make_async_copy(c_ref.at[:, pl.ds(WIDE * k, WIDE)], cot.at[k], load_sem.at[1 + k]) for k in range(5)
     ]
@@ -97,13 +109,64 @@
     ]
     for k in range(5):
         send_c[k].start()
-    load_s = pltpu.make_async_copy(state_ref, state, load_sem.at[6])
-    load_s.start()
+
+    def turn(start, core_):
+        def step(i, carry):
+            columns = pl.ds(pl.multiple_of(i * 128, 128), 128)
+            rows = pl.ds(pl.multiple_of(core_ * 1280 + i * 128, 128), 128)
+            at[rows, :] = full[pl.ds(start, 1024), columns].T
+            return carry
+
+        lax.fori_loop(0, 10, step, 0)
+
     load_a.wait()
+    turn(near_row, core)
+
+    tall[pl.ds(120, 8), :] = jnp.zeros((8, D), jnp.float32)
+    for load in load_s:
+        load.wait()
+
+    def pack(i, carry):
+        packed[pl.ds(pl.multiple_of(i * 512, 512), 512), :] = tall[:, pl.ds(pl.multiple_of(i * 512, 512), 512)].T.astype(BF)
+        return carry
+
+    lax.fori_loop(0, 10, pack, 0)
+
+    def own_state(owner):
+        return packed.at[pl.ds(pl.multiple_of(owner * BLOCK, BLOCK), BLOCK)]
+
+    def send_state(step, carry):
+        owner = (f + step) % 32
+        remote(own_state(owner), moved.at[f], s_send, s_recv, (owner, t)).start()
+        return carry
+
+    lax.fori_loop(1, 32, send_state, 0)
+    moved[f] = packed[pl.ds(pl.multiple_of(f * BLOCK, BLOCK), BLOCK), :]
     for k in range(5):
         load_c[k].wait()
-    load_s.wait()
-    send_a.wait_recv()
+
+    def spread():
+        pltpu.make_async_copy(moved.at[pl.ds(0, 31)], moved.at[pl.ds(0, 31)], s_recv).wait()
+        lane = lax.broadcasted_iota(jnp.int32, (BLOCK, 128), 1)
+
+        def half(h, carry):
+            for group in range(5):
+                value = [jnp.zeros((BLOCK, 128), jnp.float32)] * 3
+                for g in range(16):
+                    left = 40 * g - 128 * group
+                    if left <= -40 or left >= 128:
+                        continue
+                    piece = moved[h * 16 + g].astype(jnp.float32)
+                    here = (lane >= left) & (lane < left + 40)
+                    for i in range(3):
+                        shift = (left - 40 * i) % 128
+                        rolled = pltpu.roll(piece, shift, 1) if shift else piece
+                        value[i] = jnp.where(here, rolled, value[i])
+                for i in range(3):
+                    fresh[i, :, pl.ds(pl.multiple_of(h * 640 + group * 128, 128), 128)] = value[i]
+            return carry
+
+        lax.fori_loop(0, 2, half, 0)
 
     def base(color, stage):
         total = 0
@@ -180,7 +243,13 @@
                 def _(k=k):
                     send_c[k].wait_recv()
 
-            def rows(quarter, carry):
+            def rows(step, carry):
+                @pl.when((now == 0) & (step == 2))
+                def _():
+                    send_a.wait_recv()
+                    turn(near_row + 1024, 1 - core)
+
+                quarter = (core * 2 + step) % 4
                 left = at[pl.ds(pl.multiple_of(quarter * 640, 128), 640), :]
                 product = jnp.dot(left, cot[now], preferred_element_type=jnp.float32).astype(BF)
                 for i in range(4):
@@ -193,6 +262,10 @@
             for color in range(4):
                 halving(now, color, 0).start()
 
+        @pl.when(now == 7)
+        def _():
+            spread()
+
         return carry
 
     lax.fori_loop(0, WAVES + 5, tick, 0)
@@ -209,7 +282,7 @@
             rows = pl.ds((color // 2) * 80, 80)
             columns = pl.ds(pl.multiple_of(k * WIDE + (color % 2) * 128, 128), 128)
             gradient = final[0, k, color].astype(jnp.float32) + final[1, k, color].astype(jnp.float32)
-            new = adam_update(*(state[i, rows, columns].astype(jnp.float32) for i in range(3)), gradient)
+            new = adam_update(*(fresh[i, rows, columns] for i in range(3)), gradient)
             for i in range(3):
                 fresh[i, rows, columns] = new[i]
             full[pl.ds(my_rows + (color // 2) * 80, 80), columns] = new[0].astype(BF)
@@ -282,6 +355,7 @@
     store_far.start()
 
     send_a.wait_send()
+    pltpu.make_async_copy(packed.at[pl.ds(0, 4960)], packed.at[pl.ds(0, 4960)], s_send).wait()
     for k in range(5):
         send_c[k].wait_send()
     pltpu.make_async_copy(recv, recv, rs_send).wait()
@@ -301,9 +375,6 @@
 
 
 def body(activations, cotangent, weights, first_moment, second_moment):
-    packed = jnp.concatenate([weights, first_moment, second_moment], axis=1).astype(BF)
-    moved = lax.all_to_all(packed.reshape(32, BLOCK, 120), "fsdp", 0, 0, tiled=True)
-    state = moved.reshape(32, BLOCK, 3, 40).transpose(2, 1, 0, 3).reshape(3, BLOCK, 1280)
     any_space = pl.BlockSpec(memory_space=pl.ANY)
     shard = jax.ShapeDtypeStruct((BLOCK, 1280), jnp.float32)
     dma = pltpu.SemaphoreType.DMA
@@ -311,7 +382,7 @@
         kernel,
         name="step",
         out_shape=(shard, shard, shard, jax.ShapeDtypeStruct((D, 1280), BF)),
-        in_specs=[any_space] * 3,
+        in_specs=[any_space] * 5,
         out_specs=(any_space,) * 4,
         scratch_shapes=[
             pltpu.VMEM((2560, 1024), BF),
@@ -321,16 +392,18 @@
             pltpu.VMEM((WAVES, 4, 80, 128), BF),
             pltpu.VMEM((2, 5, 4, 80, 128), BF),
             pltpu.VMEM((D, 1280), BF),
-            pltpu.VMEM((3, BLOCK, 1280), BF),
             pltpu.VMEM((3, BLOCK, 1280), jnp.float32),
-            dma((7,)), dma, dma, dma((5,)), dma((5,)), dma, dma((WAVES, 4, 4)), dma((WAVES,)), dma((2, 5)),
+            pltpu.VMEM((128, D), jnp.float32),
+            pltpu.VMEM((D, 128), BF),
+            pltpu.VMEM((32, BLOCK, 128), BF),
+            dma((9,)), dma, dma, dma, dma, dma((5,)), dma((5,)), dma, dma((WAVES, 4, 4)), dma((WAVES,)), dma((2, 5)),
             dma, dma((2, 4, 16)), dma, dma, dma((5,)),
         ],
         compiler_params=pltpu.CompilerParams(
             collective_id=0, has_side_effects=True, vmem_limit_bytes=67043328
         ),
         cost_estimate=pl.CostEstimate(flops=13_421_772_800, bytes_accessed=40_000_000, transcendentals=0),
-    )(activations.T, cotangent, state)
+    )(activations, cotangent, weights.T, first_moment.T, second_moment.T)
 
 
 def solution(mesh):

time: 231 us -> 214 us (0.926)
  Pallas kernels: 167 us -> 195 us
  waiting for transfers between devices: 16 us -> 0 us
  local copies, waits for them, and re-layouts: 32.4 us -> 17 us
  starting transfers between devices: 9.89 us -> 0 us
  other arithmetic: 2.8 us -> 0 us
    pallas_call x1, Pallas kernels: 167 us -> 195 us  [body(): pl.pallas_call(kernel, name='step', out_shape=(shard, shard, shard, jax.S...]
    all_to_all x1 -> x0, waiting for transfers between devices: 16 us -> none  [body(): lax.all_to_all(packed.reshape(32, BLOCK, 120), 'fsdp', 0, 0, tiled=True)]
    all_to_all x1 -> x0, starting transfers between devices: 9.89 us -> none  [body(): lax.all_to_all(packed.reshape(32, BLOCK, 120), 'fsdp', 0, 0, tiled=True)]
    concatenate x4 -> x0, local copies, waits for them, and re-layouts: 6.08 us -> none  [body(): jnp.concatenate([weights, first_moment, second_moment], axis=1).astype(BF)]
    reshape x1 -> x0, local copies, waits for them, and re-layouts: 3.67 us -> none  [body(): moved.reshape(32, BLOCK, 3, 40).transpose(2, 1, 0, 3)]
    unnamed x13 -> x4, local copies, waits for them, and re-layouts: 19.1 us -> 17 us
  transfers between devices with their start and end apart: 1 -> 0, of which waited for: 1 -> 0; matrix products, arithmetic and copies ran while one was open for 2% -> 0% of each run, Pallas kernels for 0% -> 0%
where the time goes in v2:
time: 214 us; the launch traced here: 213 us
  Pallas kernels  195 us (91%)
  local copies, waits for them, and re-layouts  17 us (8%)
    pallas_call x1, Pallas kernels, body(): pl.pallas_call(kernel, name='step', out_shape=(shard, shard, shard, jax.S...  195 us
    unnamed x4, local copies, waits for them, and re-layouts  17 us

profile of v2, /device:TPU:2, one launch (start us, length us, event | category | flops | bytes accessed | tf_op | source)
XLA Modules:
  0.0 213.0 jit_solution(5770366505663166665)
XLA Ops:
  0.6 195.3 %step.1 = (f32[160,1280]{1,0:T(8,128)}, f32[160,1280]{1,0:T(8,128)}, f32[160,1280]{1,0:T(8,128)}, bf16[5120,1280]{1,0:T(8,128)(2,1)}) custom-call(bf16[1024,1280]{1,0:T(8,128)(2,1)} %a_ref.1, bf16[1024,1280]{1,0:T(8,128)(2,1)} %c_ref.1, f32[40,5120]{1,0:T(8,128)} %bitcast.3, f32[40,5120]{1,0:T(8,128)} %bitcast.4, f32[40,5120]{1,0:T(8,128)} %bitcast.5), custom_call_target="tpu_custom_call" | custom-call | flops 13421772800 | bytes 40000000 | tf_op jit(solution)/shard_map/step/pallas_call | solution.py:381
  195.9 2.1 copy.13
  198.0 2.1 copy.14
  200.1 2.1 copy.15
  202.2 10.7 %copy.16 = bf16[5120,1280]{1,0:T(8,128)(2,1)} copy(bf16[5120,1280]{1,0:T(8,128)(2,1)} %get-tuple-element.11) | data formatting | bytes 26214400

commit v3 on v2

--- a/solution.py
+++ b/solution.py
@@ -50,7 +50,7 @@
     a_ref, c_ref, w_ref, m_ref, v_ref, wn_out, mn_out, vn_out, full_out,
     at, cot, part, recv, summed, final, full, fresh, tall, packed, moved,
     load_sem, s_send, s_recv, a_send, a_recv, c_send, c_recv, rs_send, rs_recv, x_send, x_recv, ag_send, ag_recv,
-    gx_send, gx_recv, out_sem,
+    gx_send, out_sem,
 ):
     f, t = lax.axis_index("fsdp"), lax.axis_index("tensor")
     hi, z, y = f // 16, (f // 4) % 4, f % 4
@@ -107,8 +107,8 @@
         remote(c_ref.at[:, pl.ds(WIDE * k, WIDE)], cot.at[5 + k], c_send.at[k], c_recv.at[k], lo_peer)
         for k in range(5)
     ]
-    for k in range(5):
-        send_c[k].start()
+    send_c[0].start()
+    send_c[1].start()
 
     def turn(start, core_):
         def step(i, carry):
@@ -136,7 +136,7 @@
         return packed.at[pl.ds(pl.multiple_of(owner * BLOCK, BLOCK), BLOCK)]
 
     def send_state(step, carry):
-        owner = (f + step) % 32
+        owner = ((f // 16 + step // 16) % 2) * 16 + (f + step) % 16
         remote(own_state(owner), moved.at[f], s_send, s_recv, (owner, t)).start()
         return carry
 
@@ -204,72 +204,6 @@
         return remote(summed.at[wave], final.at[hi, k], x_send.at[wave], x_recv.at[hi, k], x_target(wave))
 
     stays = hi == lo
-
-    def tick(now, carry):
-        wave_4 = now - 5
-
-        @pl.when((wave_4 >= 0) & (wave_4 < WAVES))
-        def _():
-            for color in range(4):
-                halving(wave_4, color, 3).wait_recv()
-                summed[wave_4, color] = (
-                    part[wave_4, color, base(color, 4)].astype(jnp.float32)
-                    + recv[wave_4, color, SLOT[3]].astype(jnp.float32)
-                ).astype(BF)
-
-            @pl.when(stays & (wave_4 < 5))
-            def _():
-                final[hi, wave_4 % 5] = summed[wave_4]
-
-            @pl.when(jnp.logical_not(stays & (wave_4 < 5)))
-            def _():
-                x_copy(wave_4).start()
-
-        for stage in (3, 2, 1):
-            wave = now - 1 - stage
-
-            @pl.when((wave >= 0) & (wave < WAVES))
-            def _(wave=wave, stage=stage):
-                for color in range(4):
-                    halving(wave, color, stage - 1).wait_recv()
-                    add(wave, color, stage, 1)
-                    halving(wave, color, stage).start()
-                    add(wave, color, stage, 0)
-
-        @pl.when(now < WAVES)
-        def _():
-            for k in range(5):
-                @pl.when(now == 5 + k)
-                def _(k=k):
-                    send_c[k].wait_recv()
-
-            def rows(step, carry):
-                @pl.when((now == 0) & (step == 2))
-                def _():
-                    send_a.wait_recv()
-                    turn(near_row + 1024, 1 - core)
-
-                quarter = (core * 2 + step) % 4
-                left = at[pl.ds(pl.multiple_of(quarter * 640, 128), 640), :]
-                product = jnp.dot(left, cot[now], preferred_element_type=jnp.float32).astype(BF)
-                for i in range(4):
-                    for color in range(4):
-                        top, side = i * BLOCK + (color // 2) * 80, (color % 2) * 128
-                        part[now, color, place(color, quarter, i)] = product[top : top + 80, side : side + 128]
-                return carry
-
-            lax.fori_loop(0, 4, rows, 0)
-            for color in range(4):
-                halving(now, color, 0).start()
-
-        @pl.when(now == 7)
-        def _():
-            spread()
-
-        return carry
-
-    lax.fori_loop(0, WAVES + 5, tick, 0)
-
     my_rows = pl.multiple_of(f * BLOCK, BLOCK)
 
     def update(k, carry):
@@ -288,9 +222,7 @@
             full[pl.ds(my_rows + (color // 2) * 80, 80), columns] = new[0].astype(BF)
         return carry
 
-    lax.fori_loop(0, 5, update, 0)
-
-    def block(x, color, number):
+    def block(late, color, number):
         z_, y_ = z, y
         order = ORDER[color][::-1]
         for i in range(4):
@@ -300,59 +232,157 @@
                     y_ = flip(y_, dim)
                 else:
                     z_ = flip(z_, dim)
-        owner = ((1 - hi if x else hi) * 4 + z_) * 4 + y_
+        owner = ((1 - lo if late else lo) * 4 + z_) * 4 + y_
         rows = pl.ds(pl.multiple_of(owner * BLOCK + (color // 2) * 80, 16), 80)
         return full.at[rows, pl.ds((color % 2) * 640, 640)]
 
-    def forward(x, color, number, i):
-        here = block(x, color, number)
+    def forward(late, color, number, i):
+        here = block(late, color, number)
         return remote(
-            here, here, ag_send, ag_recv.at[x, color, number + (1 << i)], cube_peer(ORDER[color][::-1][i])
+            here, here, ag_send, ag_recv.at[late, color, number + (1 << i)], cube_peer(ORDER[color][::-1][i])
         )
 
-    def arrived(x, color, number):
-        here = block(x, color, number)
-        pltpu.make_async_copy(here, here, ag_recv.at[x, color, number]).wait()
-
-    own_rows = full.at[pl.ds(my_rows, BLOCK)]
-    to_hi = remote(own_rows, own_rows, gx_send, gx_recv, hi_peer)
-    to_hi.start()
-    for color in range(4):
-        for i in (3, 2, 1, 0):
-            forward(0, color, 0, i).start()
+    def arrived(late, color, number):
+        here = block(late, color, number)
+        pltpu.make_async_copy(here, here, ag_recv.at[late, color, number]).wait()
+
+    def to_hi(late, color):
+        here = block(late, color, 0)
+        return remote(here, here, gx_send.at[color], ag_recv.at[late, color, 0], hi_peer)
+
+    def roots(late, source):
+        for color in range(4):
+            if source:
+                to_hi(late, color).start()
+            else:
+                arrived(late, color, 0)
+            for i in (3, 2, 1, 0):
+                forward(late, color, 0, i).start()
+
+    def relay(late, number):
+        for color in range(4):
+            arrived(late, color, number)
+            for i in (3, 2, 1):
+                if number < 1 << i:
+                    forward(late, color, number, i).start()
+
+    def wave_at(now):
+        return (now >= 0) & (now < WAVES), now
+
+    def tick(now, carry):
+        valid_4, wave_4 = wave_at(now - 5)
+
+        @pl.when(valid_4)
+        def _():
+            for color in range(4):
+                halving(wave_4, color, 3).wait_recv()
+                summed[wave_4, color] = (
+                    part[wave_4, color, base(color, 4)].astype(jnp.float32)
+                    + recv[wave_4, color, SLOT[3]].astype(jnp.float32)
+                ).astype(BF)
+
+            @pl.when(stays & (wave_4 < 5))
+            def _():
+                final[hi, wave_4 % 5] = summed[wave_4]
+
+            @pl.when(jnp.logical_not(stays & (wave_4 < 5)))
+            def _():
+                x_copy(wave_4).start()
+
+        for stage in (3, 2, 1):
+            valid, wave = wave_at(now - 1 - stage)
+
+            @pl.when(valid)
+            def _(wave=wave, stage=stage):
+                for color in range(4):
+                    halving(wave, color, stage - 1).wait_recv()
+                    add(wave, color, stage, 1)
+                    halving(wave, color, stage).start()
+                    add(wave, color, stage, 0)
+
+        valid_0, wave_0 = wave_at(now)
+
+        @pl.when(valid_0)
+        def _():
+            for k in range(5):
+                @pl.when(wave_0 == 5 + k)
+                def _(k=k):
+                    send_c[k].wait_recv()
+
+            def rows(step, carry):
+                @pl.when((now == 0) & (step == 2))
+                def _():
+                    send_a.wait_recv()
+                    turn(near_row + 1024, 1 - core)
+
+                quarter = (core * 2 + step) % 4
+                left = at[pl.ds(pl.multiple_of(quarter * 640, 128), 640), :]
+                product = jnp.dot(left, cot[wave_0], preferred_element_type=jnp.float32).astype(BF)
+                for i in range(4):
+                    for color in range(4):
+                        top, side = i * BLOCK + (color // 2) * 80, (color % 2) * 128
+                        part[wave_0, color, place(color, quarter, i)] = product[top : top + 80, side : side + 128]
+                return carry
+
+            lax.fori_loop(0, 4, rows, 0)
+            for color in range(4):
+                halving(wave_0, color, 0).start()
+
+        for k, when in ((2, 1), (3, 3), (4, 4)):
+            @pl.when(now == when)
+            def _(k=k):
+                send_c[k].start()
+
+        @pl.when(now == 11)
+        def _():
+            spread()
+
+        @pl.when(stays & (now == 12))
+        def _():
+            lax.fori_loop(0, 5, update, 0)
+            roots(0, True)
+
+        @pl.when(jnp.logical_not(stays) & (now == 13))
+        def _():
+            roots(0, False)
+
+        @pl.when(now == jnp.where(stays, 13, 14))
+        def _():
+            relay(0, 1)
+
+        return carry
+
+    lax.fori_loop(0, WAVES + 5, tick, 0)
+
+    @pl.when(jnp.logical_not(stays))
+    def _():
+        lax.fori_loop(0, 5, update, 0)
+        roots(1, True)
+
+    for number in range(2, 8):
+        relay(0, number)
+
+    @pl.when(stays)
+    def _():
+        roots(1, False)
+
     stores = [
         pltpu.make_async_copy(fresh.at[i], out, out_sem.at[i]) for i, out in enumerate((wn_out, mn_out, vn_out))
     ]
     for store in stores:
         store.start()
-    for number in range(1, 8):
-        for color in range(4):
-            arrived(0, color, number)
-            for i in (3, 2, 1):
-                if number < 1 << i:
-                    forward(0, color, number, i).start()
-    to_hi.wait_recv()
-    for color in range(4):
-        for i in (3, 2, 1, 0):
-            forward(1, color, 0, i).start()
+    for number in range(1, 4):
+        relay(1, number)
     for number in range(8, 16):
-        for color in range(4):
-            arrived(0, color, number)
-    near = pl.ds(pl.multiple_of(hi * 2560, 128), 2560)
-    far = pl.ds(pl.multiple_of((1 - hi) * 2560, 128), 2560)
-    store_near = pltpu.make_async_copy(full.at[near], full_out.at[near], out_sem.at[3])
-    store_near.start()
-    for number in range(1, 8):
-        for color in range(4):
-            arrived(1, color, number)
-            for i in (3, 2, 1):
-                if number < 1 << i:
-                    forward(1, color, number, i).start()
-    for number in range(8, 16):
-        for color in range(4):
-            arrived(1, color, number)
-    store_far = pltpu.make_async_copy(full.at[far], full_out.at[far], out_sem.at[4])
-    store_far.start()
+        relay(0, number)
+    early_rows = pl.ds(pl.multiple_of(lo * 2560, 128), 2560)
+    late_rows = pl.ds(pl.multiple_of((1 - lo) * 2560, 128), 2560)
+    store_early = pltpu.make_async_copy(full.at[early_rows], full_out.at[early_rows], out_sem.at[3])
+    store_early.start()
+    for number in range(4, 16):
+        relay(1, number)
+    store_late = pltpu.make_async_copy(full.at[late_rows], full_out.at[late_rows], out_sem.at[4])
+    store_late.start()
 
     send_a.wait_send()
     pltpu.make_async_copy(packed.at[pl.ds(0, 4960)], packed.at[pl.ds(0, 4960)], s_send).wait()
@@ -366,19 +396,37 @@
                 x_copy(wave).wait_send()
         else:
             x_copy(wave).wait_send()
-    to_hi.wait_send()
+    for color in range(4):
+        to_hi(0, color).wait_send()
     pltpu.make_async_copy(full.at[pl.ds(0, 4800)], full.at[pl.ds(0, 4800)], ag_send).wait()
     for store in stores:
         store.wait()
-    store_near.wait()
-    store_far.wait()
+    store_early.wait()
+    store_late.wait()
+
+
+def copy_kernel(*refs):
+    sources, targets, (small, large, in_sem, out_sem) = refs[:4], refs[4:8], refs[8:]
+    pieces = [(sources[i], small.at[i], targets[i]) for i in range(3)]
+    for i in range(10):
+        rows = pl.ds(512 * i, 512)
+        pieces.append((sources[3].at[rows], large.at[rows], targets[3].at[rows]))
+    reads = [pltpu.make_async_copy(a, b, in_sem.at[i]) for i, (a, b, c) in enumerate(pieces)]
+    writes = [pltpu.make_async_copy(b, c, out_sem.at[i]) for i, (a, b, c) in enumerate(pieces)]
+    for read in reads:
+        read.start()
+    for read, write in zip(reads, writes):
+        read.wait()
+        write.start()
+    for write in writes:
+        write.wait()
 
 
 def body(activations, cotangent, weights, first_moment, second_moment):
     any_space = pl.BlockSpec(memory_space=pl.ANY)
     shard = jax.ShapeDtypeStruct((BLOCK, 1280), jnp.float32)
     dma = pltpu.SemaphoreType.DMA
-    return pl.pallas_call(
+    results = pl.pallas_call(
         kernel,
         name="step",
         out_shape=(shard, shard, shard, jax.ShapeDtypeStruct((D, 1280), BF)),
@@ -397,13 +445,23 @@
             pltpu.VMEM((D, 128), BF),
             pltpu.VMEM((32, BLOCK, 128), BF),
             dma((9,)), dma, dma, dma, dma, dma((5,)), dma((5,)), dma, dma((WAVES, 4, 4)), dma((WAVES,)), dma((2, 5)),
-            dma, dma((2, 4, 16)), dma, dma, dma((5,)),
+            dma, dma((2, 4, 16)), dma((4,)), dma((5,)),
         ],
         compiler_params=pltpu.CompilerParams(
             collective_id=0, has_side_effects=True, vmem_limit_bytes=67043328
         ),
         cost_estimate=pl.CostEstimate(flops=13_421_772_800, bytes_accessed=40_000_000, transcendentals=0),
     )(activations, cotangent, weights.T, first_moment.T, second_moment.T)
+    return pl.pallas_call(
+        copy_kernel,
+        name="place",
+        out_shape=(shard, shard, shard, jax.ShapeDtypeStruct((D, 1280), BF)),
+        in_specs=[any_space] * 4,
+        out_specs=(any_space,) * 4,
+        scratch_shapes=[
+            pltpu.VMEM((3, BLOCK, 1280), jnp.float32), pltpu.VMEM((D, 1280), BF), dma((13,)), dma((13,)),
+        ],
+    )(*results)
 
 
 def solution(mesh):

time: 214 us -> 186 us (0.87)
  local copies, waits for them, and re-layouts: 17 us -> 0 us
  Pallas kernels: 195 us -> 185 us
    pallas_call x1, Pallas kernels: 195 us -> 174 us  [body(): pl.pallas_call(kernel, name='step', out_shape=(shard, shard, shard, jax.S...]
    unnamed x4 -> x0, local copies, waits for them, and re-layouts: 17 us -> none
    pallas_call x0 -> x1, Pallas kernels: none -> 11.3 us  [body(): pl.pallas_call(copy_kernel, name='place', out_shape=(shard, shard, shard,...]
where the time goes in v3:
time: 186 us
  Pallas kernels  185 us (99%)
    pallas_call x1, Pallas kernels, body(): pl.pallas_call(kernel, name='step', out_shape=(shard, shard, shard, jax.S...  174 us
    pallas_call x1, Pallas kernels, body(): pl.pallas_call(copy_kernel, name='place', out_shape=(shard, shard, shard,...  11.3 us

profile of v3, /device:TPU:2, one launch (start us, length us, event | category | flops | bytes accessed | tf_op | source)
XLA Modules:
  0.0 186.0 jit_solution(5267701706647581408)
XLA Ops:
  0.6 174.0 %step.1 = (f32[160,1280]{1,0:T(8,128)}, f32[160,1280]{1,0:T(8,128)}, f32[160,1280]{1,0:T(8,128)}, bf16[5120,1280]{1,0:T(8,128)(2,1)}) custom-call(bf16[1024,1280]{1,0:T(8,128)(2,1)} %a_ref.1, bf16[1024,1280]{1,0:T(8,128)(2,1)} %c_ref.1, f32[40,5120]{1,0:T(8,128)} %bitcast.3, f32[40,5120]{1,0:T(8,128)} %bitcast.4, f32[40,5120]{1,0:T(8,128)} %bitcast.5), custom_call_target="tpu_custom_call" | custom-call | flops 13421772800 | bytes 40000000 | tf_op jit(solution)/shard_map/step/pallas_call | solution.py:429
  174.6 11.3 %place.1 = (f32[160,1280]{1,0:T(8,128)}, f32[160,1280]{1,0:T(8,128)}, f32[160,1280]{1,0:T(8,128)}, bf16[5120,1280]{1,0:T(8,128)(2,1)}) custom-call(f32[160,1280]{1,0:T(8,128)} %get-tuple-element.8.refs_0_, f32[160,1280]{1,0:T(8,128)} %get-tuple-element.9.refs_1_, f32[160,1280]{1,0:T(8,128)} %get-tuple-element.10.refs_2_, ...), custom_call_target="tpu_custom_call" | custom-call | tf_op jit(solution)/shard_map/place/pallas_call | solution.py:455

commit v4 on v3

--- a/solution.py
+++ b/solution.py
@@ -47,10 +47,10 @@
 
 
 def kernel(
-    a_ref, c_ref, w_ref, m_ref, v_ref, wn_out, mn_out, vn_out, full_out,
-    at, cot, part, recv, summed, final, full, fresh, tall, packed, moved,
+    a_ref, c_ref, w_ref, m_ref, v_ref, fresh, full,
+    at, cot, part, recv, summed, final, tall, packed, moved,
     load_sem, s_send, s_recv, a_send, a_recv, c_send, c_recv, rs_send, rs_recv, x_send, x_recv, ag_send, ag_recv,
-    gx_send, out_sem,
+    gx_send,
 ):
     f, t = lax.axis_index("fsdp"), lax.axis_index("tensor")
     hi, z, y = f // 16, (f // 4) % 4, f % 4
@@ -84,14 +84,12 @@
         return carry
 
     lax.fori_loop(1, 32, greet, 0)
-    pl.semaphore_wait(barrier, 34)
 
     near_row = pl.multiple_of(hi * 2560, 128)
     raw = [full.at[pl.ds(near_row, 1024)], full.at[pl.ds(near_row + 1024, 1024)]]
     send_a = remote(a_ref, raw[1], a_send, a_recv, core_peer)
     load_a = pltpu.make_async_copy(a_ref, raw[0], load_sem.at[0])
     load_a.start()
-    send_a.start()
     load_s = [
         pltpu.make_async_copy(ref, tall.at[pl.ds(40 * i, 40)], load_sem.at[6 + i])
         for i, ref in enumerate((w_ref, m_ref, v_ref))
@@ -107,9 +105,6 @@
         remote(c_ref.at[:, pl.ds(WIDE * k, WIDE)], cot.at[5 + k], c_send.at[k], c_recv.at[k], lo_peer)
         for k in range(5)
     ]
-    send_c[0].start()
-    send_c[1].start()
-
     def turn(start, core_):
         def step(i, carry):
             columns = pl.ds(pl.multiple_of(i * 128, 128), 128)
@@ -131,6 +126,11 @@
         return carry
 
     lax.fori_loop(0, 10, pack, 0)
+
+    pl.semaphore_wait(barrier, 34)
+    send_a.start()
+    send_c[0].start()
+    send_c[1].start()
 
     def own_state(owner):
         return packed.at[pl.ds(pl.multiple_of(owner * BLOCK, BLOCK), BLOCK)]
@@ -366,24 +366,12 @@
     def _():
         roots(1, False)
 
-    stores = [
-        pltpu.make_async_copy(fresh.at[i], out, out_sem.at[i]) for i, out in enumerate((wn_out, mn_out, vn_out))
-    ]
-    for store in stores:
-        store.start()
     for number in range(1, 4):
         relay(1, number)
     for number in range(8, 16):
         relay(0, number)
-    early_rows = pl.ds(pl.multiple_of(lo * 2560, 128), 2560)
-    late_rows = pl.ds(pl.multiple_of((1 - lo) * 2560, 128), 2560)
-    store_early = pltpu.make_async_copy(full.at[early_rows], full_out.at[early_rows], out_sem.at[3])
-    store_early.start()
     for number in range(4, 16):
         relay(1, number)
-    store_late = pltpu.make_async_copy(full.at[late_rows], full_out.at[late_rows], out_sem.at[4])
-    store_late.start()
-
     send_a.wait_send()
     pltpu.make_async_copy(packed.at[pl.ds(0, 4960)], packed.at[pl.ds(0, 4960)], s_send).wait()
     for k in range(5):
@@ -399,27 +387,17 @@
     for color in range(4):
         to_hi(0, color).wait_send()
     pltpu.make_async_copy(full.at[pl.ds(0, 4800)], full.at[pl.ds(0, 4800)], ag_send).wait()
-    for store in stores:
-        store.wait()
-    store_early.wait()
-    store_late.wait()
-
-
-def copy_kernel(*refs):
-    sources, targets, (small, large, in_sem, out_sem) = refs[:4], refs[4:8], refs[8:]
-    pieces = [(sources[i], small.at[i], targets[i]) for i in range(3)]
-    for i in range(10):
-        rows = pl.ds(512 * i, 512)
-        pieces.append((sources[3].at[rows], large.at[rows], targets[3].at[rows]))
-    reads = [pltpu.make_async_copy(a, b, in_sem.at[i]) for i, (a, b, c) in enumerate(pieces)]
-    writes = [pltpu.make_async_copy(b, c, out_sem.at[i]) for i, (a, b, c) in enumerate(pieces)]
-    for read in reads:
-        read.start()
-    for read, write in zip(reads, writes):
-        read.wait()
-        write.start()
-    for write in writes:
-        write.wait()
+
+
+def copy_kernel(fresh, full, wn_out, mn_out, vn_out, full_out, sem):
+    copies = [pltpu.make_async_copy(fresh.at[i], out, sem.at[i]) for i, out in enumerate((wn_out, mn_out, vn_out))]
+    for i in range(5):
+        rows = pl.ds(1024 * i, 1024)
+        copies.append(pltpu.make_async_copy(full.at[rows], full_out.at[rows], sem.at[3 + i]))
+    for copy in copies:
+        copy.start()
+    for copy in copies:
+        copy.wait()
 
 
 def body(activations, cotangent, weights, first_moment, second_moment):
@@ -429,9 +407,9 @@
     results = pl.pallas_call(
         kernel,
         name="step",
-        out_shape=(shard, shard, shard, jax.ShapeDtypeStruct((D, 1280), BF)),
+        out_shape=(pltpu.VMEM((3, BLOCK, 1280), jnp.float32), pltpu.VMEM((D, 1280), BF)),
         in_specs=[any_space] * 5,
-        out_specs=(any_space,) * 4,
+        out_specs=(pl.BlockSpec(memory_space=pltpu.VMEM),) * 2,
         scratch_shapes=[
             pltpu.VMEM((2560, 1024), BF),
             pltpu.VMEM((10, 1024, WIDE), BF),
@@ -439,16 +417,14 @@
             pltpu.VMEM((WAVES, 4, 15, 80, 128), BF),
             pltpu.VMEM((WAVES, 4, 80, 128), BF),
             pltpu.VMEM((2, 5, 4, 80, 128), BF),
-            pltpu.VMEM((D, 1280), BF),
-            pltpu.VMEM((3, BLOCK, 1280), jnp.float32),
             pltpu.VMEM((128, D), jnp.float32),
             pltpu.VMEM((D, 128), BF),
             pltpu.VMEM((32, BLOCK, 128), BF),
             dma((9,)), dma, dma, dma, dma, dma((5,)), dma((5,)), dma, dma((WAVES, 4, 4)), dma((WAVES,)), dma((2, 5)),
-            dma, dma((2, 4, 16)), dma((4,)), dma((5,)),
+            dma, dma((2, 4, 16)), dma((4,)),
         ],
         compiler_params=pltpu.CompilerParams(
-            collective_id=0, has_side_effects=True, vmem_limit_bytes=67043328
+            collective_id=0, has_side_effects=True, vmem_limit_bytes=46 << 20
         ),
         cost_estimate=pl.CostEstimate(flops=13_421_772_800, bytes_accessed=40_000_000, transcendentals=0),
     )(activations, cotangent, weights.T, first_moment.T, second_moment.T)
@@ -456,11 +432,10 @@
         copy_kernel,
         name="place",
         out_shape=(shard, shard, shard, jax.ShapeDtypeStruct((D, 1280), BF)),
-        in_specs=[any_space] * 4,
+        in_specs=[pl.BlockSpec(memory_space=pltpu.VMEM)] * 2,
         out_specs=(any_space,) * 4,
-        scratch_shapes=[
-            pltpu.VMEM((3, BLOCK, 1280), jnp.float32), pltpu.VMEM((D, 1280), BF), dma((13,)), dma((13,)),
-        ],
+        scratch_shapes=[dma((8,))],
+        compiler_params=pltpu.CompilerParams(vmem_limit_bytes=1 << 20),
     )(*results)
 
 

time: 186 us -> 177 us (0.952)
  Pallas kernels: 185 us -> 177 us
    pallas_call x1, Pallas kernels: 11.3 us -> 5.6 us  [body(): pl.pallas_call(copy_kernel, name='place', out_shape=(shard, shard, shard,...]
    pallas_call x1, Pallas kernels: 174 us -> 171 us  [body(): pl.pallas_call(kernel, name='step', out_shape=(pltpu.VMEM((3, BLOCK, 1280...]
where the time goes in v4:
time: 177 us
  Pallas kernels  177 us (100%)
    pallas_call x1, Pallas kernels, body(): pl.pallas_call(kernel, name='step', out_shape=(pltpu.VMEM((3, BLOCK, 1280...  171 us
    pallas_call x1, Pallas kernels, body(): pl.pallas_call(copy_kernel, name='place', out_shape=(shard, shard, shard,...  5.6 us

profile of v4, /device:TPU:2, one launch (start us, length us, event | category | flops | bytes accessed | tf_op | source)
XLA Modules:
  0.0 177.3 jit_solution(14255051390461843836)
XLA Ops:
  0.6 171.0 %step.1 = (f32[3,160,1280]{2,1,0:T(8,128)S(1)}, bf16[5120,1280]{1,0:T(8,128)(2,1)S(1)}) custom-call(bf16[1024,1280]{1,0:T(8,128)(2,1)} %a_ref.1, bf16[1024,1280]{1,0:T(8,128)(2,1)} %c_ref.1, f32[40,5120]{1,0:T(8,128)} %bitcast.3, f32[40,5120]{1,0:T(8,128)} %bitcast.4, f32[40,5120]{1,0:T(8,128)} %bitcast.5), custom_call_target="tpu_custom_call" | custom-call | flops 13421772800 | bytes 40000000 | tf_op jit(solution)/shard_map/step/pallas_call | solution.py:407
  171.7 5.6 %place.1 = (f32[160,1280]{1,0:T(8,128)}, f32[160,1280]{1,0:T(8,128)}, f32[160,1280]{1,0:T(8,128)}, bf16[5120,1280]{1,0:T(8,128)(2,1)}) custom-call(f32[3,160,1280]{2,1,0:T(8,128)S(1)} %get-tuple-element.6.fresh, bf16[5120,1280]{1,0:T(8,128)(2,1)S(1)} %get-tuple-element.7.full), custom_call_target="tpu_custom_call" | custom-call | tf_op jit(solution)/shard_map/place/pallas_call | solution.py:431

commit v5 on v4

--- a/solution.py
+++ b/solution.py
@@ -10,6 +10,7 @@
 BLOCK = 160
 WAVES = 10
 WIDE = 256
+SIDE = (256, 128)
 MESH = pl.DeviceIdType.MESH
 BF = jnp.bfloat16
 
@@ -50,7 +51,7 @@
     a_ref, c_ref, w_ref, m_ref, v_ref, fresh, full,
     at, cot, part, recv, summed, final, tall, packed, moved,
     load_sem, s_send, s_recv, a_send, a_recv, c_send, c_recv, rs_send, rs_recv, x_send, x_recv, ag_send, ag_recv,
-    gx_send,
+    gx_send, side_send, side_recv,
 ):
     f, t = lax.axis_index("fsdp"), lax.axis_index("tensor")
     hi, z, y = f // 16, (f // 4) % 4, f % 4
@@ -129,8 +130,8 @@
 
     pl.semaphore_wait(barrier, 34)
     send_a.start()
-    send_c[0].start()
-    send_c[1].start()
+    for k in range(5):
+        send_c[k].start()
 
     def own_state(owner):
         return packed.at[pl.ds(pl.multiple_of(owner * BLOCK, BLOCK), BLOCK)]
@@ -140,7 +141,7 @@
         remote(own_state(owner), moved.at[f], s_send, s_recv, (owner, t)).start()
         return carry
 
-    lax.fori_loop(1, 32, send_state, 0)
+    lax.fori_loop(1, 16, send_state, 0)
     moved[f] = packed[pl.ds(pl.multiple_of(f * BLOCK, BLOCK), BLOCK), :]
     for k in range(5):
         load_c[k].wait()
@@ -222,7 +223,7 @@
             full[pl.ds(my_rows + (color // 2) * 80, 80), columns] = new[0].astype(BF)
         return carry
 
-    def block(late, color, number):
+    def block(late, color, number, piece):
         z_, y_ = z, y
         order = ORDER[color][::-1]
         for i in range(4):
@@ -234,37 +235,65 @@
                     z_ = flip(z_, dim)
         owner = ((1 - lo if late else lo) * 4 + z_) * 4 + y_
         rows = pl.ds(pl.multiple_of(owner * BLOCK + (color // 2) * 80, 16), 80)
-        return full.at[rows, pl.ds((color % 2) * 640, 640)]
-
-    def forward(late, color, number, i):
-        here = block(late, color, number)
-        return remote(
-            here, here, ag_send, ag_recv.at[late, color, number + (1 << i)], cube_peer(ORDER[color][::-1][i])
-        )
-
-    def arrived(late, color, number):
-        here = block(late, color, number)
-        pltpu.make_async_copy(here, here, ag_recv.at[late, color, number]).wait()
+        start = (color % 2) * 640
+        columns = {
+            "all": (start, 640), "main": (start, 640 - SIDE[late]), "side": (start + 640 - SIDE[late], SIDE[late])
+        }[piece]
+        return full.at[rows, pl.ds(*columns)]
+
+    def landing(late, color, number, piece):
+        return rs_recv.at[number // 4, number % 4, color] if piece == "side" else ag_recv.at[late, color, number]
+
+    def forward(late, color, number, i, piece):
+        here = block(late, color, number, piece)
+        there = landing(late, color, number + (1 << i), piece)
+        return remote(here, here, ag_send, there, cube_peer(ORDER[color][::-1][i]))
+
+    def arrived(late, color, number, piece):
+        here = block(late, color, number, piece)
+        pltpu.make_async_copy(here, here, landing(late, color, number, piece)).wait()
 
     def to_hi(late, color):
-        here = block(late, color, 0)
+        here = block(late, color, 0, "main")
         return remote(here, here, gx_send.at[color], ag_recv.at[late, color, 0], hi_peer)
 
-    def roots(late, source):
-        for color in range(4):
-            if source:
-                to_hi(late, color).start()
-            else:
-                arrived(late, color, 0)
-            for i in (3, 2, 1, 0):
-                forward(late, color, 0, i).start()
-
-    def relay(late, number):
-        for color in range(4):
-            arrived(late, color, number)
+    def side(late, color, number):
+        here = block(late, color, number, "side")
+        return remote(here, here, side_send, side_recv, hi_peer)
+
+    def roots(late, color, piece):
+        for i in (3, 2, 1, 0):
+            forward(late, color, 0, i, piece).start()
+
+    def relay(late, number, piece, across):
+        for color in range(4):
+            arrived(late, color, number, piece)
             for i in (3, 2, 1):
                 if number < 1 << i:
-                    forward(late, color, number, i).start()
+                    forward(late, color, number, i, piece).start()
+            if across:
+                side(late, color, number).start()
+
+    def early_roots():
+        for color in range(4):
+            to_hi(0, color).start()
+            roots(0, color, "all")
+        for color in range(4):
+            side(0, color, 0).start()
+
+    def late_roots():
+        for color in range(4):
+            to_hi(1, color).start()
+        for color in range(4):
+            roots(1, color, "side")
+            side(1, color, 0).start()
+        for color in range(4):
+            roots(1, color, "main")
+
+    def other_roots(late):
+        for color in range(4):
+            arrived(late, color, 0, "main")
+            roots(late, color, "main")
 
     def wave_at(now):
         return (now >= 0) & (now < WAVES), now
@@ -328,10 +357,9 @@
             for color in range(4):
                 halving(wave_0, color, 0).start()
 
-        for k, when in ((2, 1), (3, 3), (4, 4)):
-            @pl.when(now == when)
-            def _(k=k):
-                send_c[k].start()
+        @pl.when(now == 4)
+        def _():
+            lax.fori_loop(16, 32, send_state, 0)
 
         @pl.when(now == 11)
         def _():
@@ -340,38 +368,59 @@
         @pl.when(stays & (now == 12))
         def _():
             lax.fori_loop(0, 5, update, 0)
-            roots(0, True)
+            early_roots()
 
         @pl.when(jnp.logical_not(stays) & (now == 13))
         def _():
-            roots(0, False)
-
-        @pl.when(now == jnp.where(stays, 13, 14))
-        def _():
-            relay(0, 1)
+            other_roots(0)
+
+        @pl.when(stays & (now == 13))
+        def _():
+            relay(0, 1, "all", True)
+
+        @pl.when(jnp.logical_not(stays) & (now == 14))
+        def _():
+            relay(0, 1, "main", False)
 
         return carry
 
     lax.fori_loop(0, WAVES + 5, tick, 0)
+
+    def arrived_across(late):
+        rows = full.at[pl.ds(0, SIDE[late] * 4)]
+        pltpu.make_async_copy(rows, rows, side_recv).wait()
+
+    @pl.when(stays)
+    def _():
+        for number in range(2, 8):
+            relay(0, number, "all", True)
+        other_roots(1)
+        for number in range(8, 16):
+            relay(0, number, "all", True)
+        for number in range(1, 16):
+            relay(1, number, "main", False)
+        arrived_across(1)
 
     @pl.when(jnp.logical_not(stays))
     def _():
         lax.fori_loop(0, 5, update, 0)
-        roots(1, True)
-
-    for number in range(2, 8):
-        relay(0, number)
-
-    @pl.when(stays)
-    def _():
-        roots(1, False)
-
-    for number in range(1, 4):
-        relay(1, number)
-    for number in range(8, 16):
-        relay(0, number)
-    for number in range(4, 16):
-        relay(1, number)
+        late_roots()
+        for number in range(2, 4):
+            relay(0, number, "main", False)
+        for number in range(1, 4):
+            relay(1, number, "side", True)
+        for number in range(4, 8):
+            relay(0, number, "main", False)
+        for number in range(4, 16):
+            relay(1, number, "side", True)
+        for number in range(1, 4):
+            relay(1, number, "main", False)
+        for number in range(8, 16):
+            relay(0, number, "main", False)
+        for number in range(4, 16):
+            relay(1, number, "main", False)
+        arrived_across(0)
+
     send_a.wait_send()
     pltpu.make_async_copy(packed.at[pl.ds(0, 4960)], packed.at[pl.ds(0, 4960)], s_send).wait()
     for k in range(5):
@@ -384,9 +433,15 @@
                 x_copy(wave).wait_send()
         else:
             x_copy(wave).wait_send()
-    for color in range(4):
-        to_hi(0, color).wait_send()
-    pltpu.make_async_copy(full.at[pl.ds(0, 4800)], full.at[pl.ds(0, 4800)], ag_send).wait()
+    for late in range(2):
+        @pl.when(stays if late == 0 else jnp.logical_not(stays))
+        def _(late=late):
+            for color in range(4):
+                to_hi(late, color).wait_send()
+            side_rows = full.at[pl.ds(0, SIDE[late] * 4)]
+            pltpu.make_async_copy(side_rows, side_rows, side_send).wait()
+            tree_rows = full.at[pl.ds(0, 60 * 80 * (1280 - SIDE[1 - late]) // 1280)]
+            pltpu.make_async_copy(tree_rows, tree_rows, ag_send).wait()
 
 
 def copy_kernel(fresh, full, wn_out, mn_out, vn_out, full_out, sem):
@@ -421,7 +476,7 @@
             pltpu.VMEM((D, 128), BF),
             pltpu.VMEM((32, BLOCK, 128), BF),
             dma((9,)), dma, dma, dma, dma, dma((5,)), dma((5,)), dma, dma((WAVES, 4, 4)), dma((WAVES,)), dma((2, 5)),
-            dma, dma((2, 4, 16)), dma((4,)),
+            dma, dma((2, 4, 16)), dma((4,)), dma, dma,
         ],
         compiler_params=pltpu.CompilerParams(
             collective_id=0, has_side_effects=True, vmem_limit_bytes=46 << 20

time: 177 us -> 169 us (0.955)
  Pallas kernels: 177 us -> 168 us
    pallas_call x1, Pallas kernels: 171 us -> 163 us  [body(): pl.pallas_call(kernel, name='step', out_shape=(pltpu.VMEM((3, BLOCK, 1280...]
where the time goes in v5:
time: 169 us
  Pallas kernels  168 us (99%)
    pallas_call x1, Pallas kernels, body(): pl.pallas_call(kernel, name='step', out_shape=(pltpu.VMEM((3, BLOCK, 1280...  163 us
    pallas_call x1, Pallas kernels, body(): pl.pallas_call(copy_kernel, name='place', out_shape=(shard, shard, shard,...  5.6 us

profile of v5, /device:TPU:2, one launch (start us, length us, event | category | flops | bytes accessed | tf_op | source)
XLA Modules:
  0.0 169.1 jit_solution(9611058706388284945)
XLA Ops:
  0.6 162.8 %step.1 = (f32[3,160,1280]{2,1,0:T(8,128)S(1)}, bf16[5120,1280]{1,0:T(8,128)(2,1)S(1)}) custom-call(bf16[1024,1280]{1,0:T(8,128)(2,1)} %a_ref.1, bf16[1024,1280]{1,0:T(8,128)(2,1)} %c_ref.1, f32[40,5120]{1,0:T(8,128)} %bitcast.3, f32[40,5120]{1,0:T(8,128)} %bitcast.4, f32[40,5120]{1,0:T(8,128)} %bitcast.5), custom_call_target="tpu_custom_call" | custom-call | flops 13421772800 | bytes 40000000 | tf_op jit(solution)/shard_map/step/pallas_call | solution.py:462
  163.5 5.6 %place.1 = (f32[160,1280]{1,0:T(8,128)}, f32[160,1280]{1,0:T(8,128)}, f32[160,1280]{1,0:T(8,128)}, bf16[5120,1280]{1,0:T(8,128)(2,1)}) custom-call(f32[3,160,1280]{2,1,0:T(8,128)S(1)} %get-tuple-element.6.fresh, bf16[5120,1280]{1,0:T(8,128)(2,1)S(1)} %get-tuple-element.7.full), custom_call_target="tpu_custom_call" | custom-call | tf_op jit(solution)/shard_map/place/pallas_call | solution.py:486

commit v6 on v5

--- a/solution.py
+++ b/solution.py
@@ -10,7 +10,7 @@
 BLOCK = 160
 WAVES = 10
 WIDE = 256
-SIDE = (256, 128)
+SIDE = ((256, 256, 128, 128), (256, 256, 128, 128))
 MESH = pl.DeviceIdType.MESH
 BF = jnp.bfloat16
 
@@ -235,9 +235,9 @@
                     z_ = flip(z_, dim)
         owner = ((1 - lo if late else lo) * 4 + z_) * 4 + y_
         rows = pl.ds(pl.multiple_of(owner * BLOCK + (color // 2) * 80, 16), 80)
-        start = (color % 2) * 640
+        start, width = (color % 2) * 640, SIDE[late][color]
         columns = {
-            "all": (start, 640), "main": (start, 640 - SIDE[late]), "side": (start + 640 - SIDE[late], SIDE[late])
+            "all": (start, 640), "main": (start, 640 - width), "side": (start + 640 - width, width)
         }[piece]
         return full.at[rows, pl.ds(*columns)]
 
@@ -274,21 +274,12 @@
             if across:
                 side(late, color, number).start()
 
-    def early_roots():
-        for color in range(4):
-            to_hi(0, color).start()
-            roots(0, color, "all")
-        for color in range(4):
-            side(0, color, 0).start()
-
     def late_roots():
         for color in range(4):
             to_hi(1, color).start()
         for color in range(4):
             roots(1, color, "side")
             side(1, color, 0).start()
-        for color in range(4):
-            roots(1, color, "main")
 
     def other_roots(late):
         for color in range(4):
@@ -361,21 +352,34 @@
         def _():
             lax.fori_loop(16, 32, send_state, 0)
 
-        @pl.when(now == 11)
+        @pl.when(now == 10)
         def _():
             spread()
 
+        @pl.when(stays & (now == 11))
+        def _():
+            lax.fori_loop(0, 5, update, 0)
+            for color in range(4):
+                to_hi(0, color).start()
+            for color in range(4):
+                side(0, color, 0).start()
+            roots(0, 0, "all")
+
+        @pl.when(jnp.logical_not(stays) & (now == 13))
+        def _():
+            other_roots(0)
+
         @pl.when(stays & (now == 12))
         def _():
-            lax.fori_loop(0, 5, update, 0)
-            early_roots()
-
-        @pl.when(jnp.logical_not(stays) & (now == 13))
-        def _():
-            other_roots(0)
+            roots(0, 1, "all")
 
         @pl.when(stays & (now == 13))
         def _():
+            for color in range(2, 4):
+                roots(0, color, "all")
+
+        @pl.when(stays & (now == 14))
+        def _():
             relay(0, 1, "all", True)
 
         @pl.when(jnp.logical_not(stays) & (now == 14))
@@ -387,7 +391,7 @@
     lax.fori_loop(0, WAVES + 5, tick, 0)
 
     def arrived_across(late):
-        rows = full.at[pl.ds(0, SIDE[late] * 4)]
+        rows = full.at[pl.ds(0, sum(SIDE[late]))]
         pltpu.make_async_copy(rows, rows, side_recv).wait()
 
     @pl.when(stays)
@@ -407,11 +411,13 @@
         late_roots()
         for number in range(2, 4):
             relay(0, number, "main", False)
-        for number in range(1, 4):
+        for number in range(1, 8):
             relay(1, number, "side", True)
+        for color in range(4):
+            roots(1, color, "main")
         for number in range(4, 8):
             relay(0, number, "main", False)
-        for number in range(4, 16):
+        for number in range(8, 16):
             relay(1, number, "side", True)
         for number in range(1, 4):
             relay(1, number, "main", False)
@@ -438,9 +444,9 @@
         def _(late=late):
             for color in range(4):
                 to_hi(late, color).wait_send()
-            side_rows = full.at[pl.ds(0, SIDE[late] * 4)]
+            side_rows = full.at[pl.ds(0, sum(SIDE[late]))]
             pltpu.make_async_copy(side_rows, side_rows, side_send).wait()
-            tree_rows = full.at[pl.ds(0, 60 * 80 * (1280 - SIDE[1 - late]) // 1280)]
+            tree_rows = full.at[pl.ds(0, 15 * 80 * (5120 - sum(SIDE[1 - late])) // 1280)]
             pltpu.make_async_copy(tree_rows, tree_rows, ag_send).wait()
 
 

time: 169 us -> 165 us (0.976)
  Pallas kernels: 168 us -> 164 us
    pallas_call x1, Pallas kernels: 163 us -> 158 us  [body(): pl.pallas_call(kernel, name='step', out_shape=(pltpu.VMEM((3, BLOCK, 1280...]
where the time goes in v6:
time: 165 us; the launch traced here: 164 us
  Pallas kernels  164 us (99%)
    pallas_call x1, Pallas kernels, body(): pl.pallas_call(kernel, name='step', out_shape=(pltpu.VMEM((3, BLOCK, 1280...  158 us
    pallas_call x1, Pallas kernels, body(): pl.pallas_call(copy_kernel, name='place', out_shape=(shard, shard, shard,...  5.6 us

profile of v6, /device:TPU:2, one launch (start us, length us, event | category | flops | bytes accessed | tf_op | source)
XLA Modules:
  0.0 164.1 jit_solution(13786961871159834435)
XLA Ops:
  0.6 157.9 %step.1 = (f32[3,160,1280]{2,1,0:T(8,128)S(1)}, bf16[5120,1280]{1,0:T(8,128)(2,1)S(1)}) custom-call(bf16[1024,1280]{1,0:T(8,128)(2,1)} %a_ref.1, bf16[1024,1280]{1,0:T(8,128)(2,1)} %c_ref.1, f32[40,5120]{1,0:T(8,128)} %bitcast.3, f32[40,5120]{1,0:T(8,128)} %bitcast.4, f32[40,5120]{1,0:T(8,128)} %bitcast.5), custom_call_target="tpu_custom_call" | custom-call | flops 13421772800 | bytes 40000000 | tf_op jit(solution)/shard_map/step/pallas_call | solution.py:468
  158.5 5.6 %place.1 = (f32[160,1280]{1,0:T(8,128)}, f32[160,1280]{1,0:T(8,128)}, f32[160,1280]{1,0:T(8,128)}, bf16[5120,1280]{1,0:T(8,128)(2,1)}) custom-call(f32[3,160,1280]{2,1,0:T(8,128)S(1)} %get-tuple-element.6.fresh, bf16[5120,1280]{1,0:T(8,128)(2,1)S(1)} %get-tuple-element.7.full), custom_call_target="tpu_custom_call" | custom-call | tf_op jit(solution)/shard_map/place/pallas_call | solution.py:492

commit v7 on v6

--- a/solution.py
+++ b/solution.py
@@ -242,7 +242,9 @@
         return full.at[rows, pl.ds(*columns)]
 
     def landing(late, color, number, piece):
-        return rs_recv.at[number // 4, number % 4, color] if piece == "side" else ag_recv.at[late, color, number]
+        if late and piece != "side":
+            return ag_recv.at[color, number]
+        return rs_recv.at[(4 if late else 0) + number // 4, number % 4, color]
 
     def forward(late, color, number, i, piece):
         here = block(late, color, number, piece)
@@ -255,7 +257,7 @@
 
     def to_hi(late, color):
         here = block(late, color, 0, "main")
-        return remote(here, here, gx_send.at[color], ag_recv.at[late, color, 0], hi_peer)
+        return remote(here, here, gx_send.at[color], landing(late, color, 0, "main"), hi_peer)
 
     def side(late, color, number):
         here = block(late, color, number, "side")
@@ -482,7 +484,7 @@
             pltpu.VMEM((D, 128), BF),
             pltpu.VMEM((32, BLOCK, 128), BF),
             dma((9,)), dma, dma, dma, dma, dma((5,)), dma((5,)), dma, dma((WAVES, 4, 4)), dma((WAVES,)), dma((2, 5)),
-            dma, dma((2, 4, 16)), dma((4,)), dma, dma,
+            dma, dma((4, 16)), dma((4,)), dma, dma,
         ],
         compiler_params=pltpu.CompilerParams(
             collective_id=0, has_side_effects=True, vmem_limit_bytes=46 << 20

time: 165 us -> 164 us (level)
  no operation moved by 1% of the time
where the time goes in v7:
time: 164 us
  Pallas kernels  163 us (99%)
    pallas_call x1, Pallas kernels, body(): pl.pallas_call(kernel, name='step', out_shape=(pltpu.VMEM((3, BLOCK, 1280...  157 us
    pallas_call x1, Pallas kernels, body(): pl.pallas_call(copy_kernel, name='place', out_shape=(shard, shard, shard,...  5.6 us

profile of v7, /device:TPU:2, one launch (start us, length us, event | category | flops | bytes accessed | tf_op | source)
XLA Modules:
  0.0 163.6 jit_solution(9083008425514591507)
XLA Ops:
  0.6 157.3 %step.1 = (f32[3,160,1280]{2,1,0:T(8,128)S(1)}, bf16[5120,1280]{1,0:T(8,128)(2,1)S(1)}) custom-call(bf16[1024,1280]{1,0:T(8,128)(2,1)} %a_ref.1, bf16[1024,1280]{1,0:T(8,128)(2,1)} %c_ref.1, f32[40,5120]{1,0:T(8,128)} %bitcast.3, f32[40,5120]{1,0:T(8,128)} %bitcast.4, f32[40,5120]{1,0:T(8,128)} %bitcast.5), custom_call_target="tpu_custom_call" | custom-call | flops 13421772800 | bytes 40000000 | tf_op jit(solution)/shard_map/step/pallas_call | solution.py:470
  158.0 5.6 %place.1 = (f32[160,1280]{1,0:T(8,128)}, f32[160,1280]{1,0:T(8,128)}, f32[160,1280]{1,0:T(8,128)}, bf16[5120,1280]{1,0:T(8,128)(2,1)}) custom-call(f32[3,160,1280]{2,1,0:T(8,128)S(1)} %get-tuple-element.6.fresh, bf16[5120,1280]{1,0:T(8,128)(2,1)S(1)} %get-tuple-element.7.full), custom_call_target="tpu_custom_call" | custom-call | tf_op jit(solution)/shard_map/place/pallas_call | solution.py:494
